TPU v7x, 32 devices: a whole 2x2x4 slice. The times are simulated.
32 devices in a mesh: row: 8 (over z, x), col: 4 (over y, core).
Axes of the slice: x: 2, y: 2, z: 4, core: 2. Of those that a mesh axis runs over, the one named last changes fastest.
Arguments:
- tensor: float32 [32, 1024, 1024], P(None, 'row', 'col'), may hold values from -6 to 6
- initial_first: float32 [1024, 256], P('row'), may hold values from -6 to 6
- initial_second: float32 [1024, 256], P('col'), may hold values from -6 to 6
Outputs:
- factor_first: float32 [1024, 256], P('row')
- factor_second: float32 [1024, 256], P('col')
- factor_frames: float32 [32, 256], replicated
- weights: float32 [256], replicated
All inputs are finite; a program needn't handle non-finite values.
Results may differ from a plain program's by a relative error of at most 0.00024.
Values sent between devices are 32-bit elements; how exact they have to be, the bound alone decides.
A program may use at most 128 MiB of HBM per device.

v0:
```python
import math

import jax
import jax.numpy as jnp
from jax import lax
from jax.sharding import PartitionSpec as P

PASSES = 2


epsilon = 1e-06


def solve_gram(partials, hadamard):
    factor_lower = jnp.linalg.cholesky(hadamard)
    midway = lax.linalg.triangular_solve(
        factor_lower, partials, left_side=False, lower=True, transpose_a=True
    )
    return lax.linalg.triangular_solve(
        factor_lower, midway, left_side=False, lower=True, transpose_a=False
    )


def local_gram(matrix):
    return jnp.dot(matrix.T, matrix, precision=lax.Precision.HIGHEST)


def normalize_second(unscaled, row_count):
    squares = lax.psum(jnp.sum(unscaled * unscaled, axis=0), "col")
    scaling = jnp.sqrt(squares / row_count + epsilon)
    normed = unscaled / scaling
    gram_new = lax.psum(local_gram(normed), "col") / row_count
    return (normed, gram_new)


def body(tensor, initial_first, initial_second):
    highest = lax.Precision.HIGHEST
    frames = tensor.shape[0]
    rows_first = tensor.shape[1] * lax.axis_size("row")
    rows_second = tensor.shape[2] * lax.axis_size("col")
    first_gram = lax.psum(local_gram(initial_first), "row") / rows_first
    second = initial_second
    second_gram = lax.psum(local_gram(initial_second), "col") / rows_second
    contracted = jnp.einsum("kij,ir->kjr", tensor, initial_first, precision=highest)
    for repeat in range(PASSES):
        frame_terms = jnp.einsum("kjr,jr->kr", contracted, second, precision=highest)
        frame_sums = lax.psum(frame_terms, ("row", "col"))
        frame_raw = solve_gram(frame_sums, first_gram * second_gram) / math.sqrt(
            rows_first * rows_second
        )
        frame_scaling = jnp.sqrt(jnp.mean(frame_raw * frame_raw, axis=0) + epsilon)
        factor_frames = frame_raw / frame_scaling
        frame_gram = local_gram(factor_frames) / frames
        second_terms = jnp.einsum("kjr,kr->jr", contracted, factor_frames, precision=highest)
        hadamard = first_gram * frame_gram
        own_rows = lax.psum_scatter(second_terms, "row", scatter_dimension=0, tiled=True)
        solved_rows = solve_gram(own_rows, hadamard) / math.sqrt(rows_first * frames)
        second_raw = lax.all_gather(solved_rows, "row", axis=0, tiled=True)
        second, second_gram = normalize_second(second_raw, rows_second)
    second_contracted = jnp.einsum("kij,jr->kir", tensor, second, precision=highest)
    first_terms = jnp.einsum("kir,kr->ir", second_contracted, factor_frames, precision=highest)
    hadamard = second_gram * frame_gram
    own_rows = lax.psum_scatter(first_terms, "col", scatter_dimension=0, tiled=True)
    solved_rows = solve_gram(own_rows, hadamard) / math.sqrt(rows_second * frames)
    first_raw = lax.all_gather(solved_rows, "col", axis=0, tiled=True)
    squares = lax.psum(jnp.sum(first_raw * first_raw, axis=0), "row")
    weights = jnp.sqrt(squares / rows_first + epsilon)
    factor_first = first_raw / weights
    return (factor_first, second, factor_frames, weights)


def solution(mesh):
    placed = (P(None, "row", "col"), P("row", None), P("col", None))
    return jax.shard_map(
        body,
        mesh=mesh,
        in_specs=placed,
        out_specs=(P("row", None), P("col", None), P(), P()),
        check_vma=False,
    )
```

profile of v0, /device:TPU:0, one launch (start us, length us, event | category | flops | bytes accessed | tf_op | source)
XLA Modules:
  0.0 647.6 jit_solution(8311122888523446965)
XLA Ops:
  10.9 10.7 %multiply_reduce_fusion.3 = (f32[256,32]{0,1:T(8,128)S(1)}, f32[32,256,256]{2,1,0:T(8,128)}) fusion(f32[256,256]{0,1:T(8,128)} %bitcast.270, f32[32,128,256]{2,1,0:T(8,128)} %param.8, f32[128,256]{1,0:T(8,128)S(1)} %copy-done), kind=kOutput, calls=%fused_computation.13 | convolution fusion | flops 3225411584 | bytes 13008896 | tf_op jit(solution)/shard_map/kij,ir->kjr/dot_general | solution.py:44
  21.7 43.2 %psum.65 = f32[32,256]{0,1:T(8,128)S(1)} all-reduce(f32[32,256]{0,1:T(8,128)S(1)} %bitcast.276), channel_id=1, replica_groups=mesh['row'=8,'col'=4] {'row','col'}, use_global_device_ids=true, to_apply=%region_6.0 | all-reduce | flops 8192 | bytes 65536 | tf_op jit(solution)/shard_map/psum | solution.py:47
  65.0 55.4 %all-reduce.6.cloned.1.call-done = f32[256,256]{0,1:T(8,128)} async-done(((f32[256,256]{0,1:T(8,128)}), f32[256,256]{0,1:T(8,128)}) %all-reduce.6.cloned.1.call-update) | async-done | bytes 262160 | tf_op jit(solution)/shard_map/psum | solution.py:41
  121.7 11.7 %cholesky.256 = f32[128,128]{1,0:T(8,128)S(1)} custom-call(f32[128,128]{1,0:T(8,128)S(1)} %cholesky.422), custom_call_target="Cholesky" | custom-call | tf_op jit(solution)/shard_map/jit(cholesky)/cholesky | solution.py:15
  143.8 11.7 %cholesky.273 = f32[128,128]{1,0:T(8,128)S(1)} custom-call(f32[128,128]{1,0:T(8,128)S(1)} %convolution_subtract_fusion.9), custom_call_target="Cholesky" | custom-call | tf_op jit(solution)/shard_map/jit(cholesky)/cholesky | solution.py:15
  161.6 20.1 %custom-call.27 = f32[2,128,128]{1,2,0:T(8,128)S(1)} custom-call(f32[2,128,128]{2,1,0:T(8,128)S(1)} %get-tuple-element.71), custom_call_target="InvertDiagBlocksLowerTriangular" | custom-call | tf_op jit(solution)/shard_map/triangular_solve/custom-call.0 | solution.py:16
  188.7 11.7 %cholesky.290 = f32[128,128]{1,0:T(8,128)S(1)} custom-call(f32[128,128]{1,0:T(8,128)S(1)} %cholesky.425), custom_call_target="Cholesky" | custom-call | tf_op jit(solution)/shard_map/jit(cholesky)/cholesky | solution.py:15
  210.8 11.7 %cholesky.307 = f32[128,128]{1,0:T(8,128)S(1)} custom-call(f32[128,128]{1,0:T(8,128)S(1)} %convolution_subtract_fusion.7), custom_call_target="Cholesky" | custom-call | tf_op jit(solution)/shard_map/jit(cholesky)/cholesky | solution.py:15
  229.3 19.7 %custom-call.30 = f32[2,128,128]{1,2,0:T(8,128)S(1)} custom-call(f32[2,128,128]{2,1,0:T(8,128)S(1)} %get-tuple-element.73), custom_call_target="InvertDiagBlocksLowerTriangular" | custom-call | tf_op jit(solution)/shard_map/triangular_solve/custom-call.0 | solution.py:16
  252.6 30.9 %all_gather.9 = f32[256,256]{1,0:T(8,128)S(1)} all-gather(f32[32,256]{1,0:T(8,128)S(1)} %maximum_multiply_fusion.1), channel_id=1, replica_groups=mesh['row'=8,'col'=4] {'row'}, dimensions={0}, use_global_device_ids=true | all-gather | bytes 294912 | tf_op jit(solution)/shard_map/all_gather | solution.py:58
  294.9 39.1 %psum.68 = f32[32,256]{0,1:T(8,128)S(1)} all-reduce(f32[32,256]{0,1:T(8,128)S(1)} %bitcast.277), channel_id=1, replica_groups=mesh['row'=8,'col'=4] {'row','col'}, use_global_device_ids=true, to_apply=%region_12.16 | all-reduce | flops 8192 | bytes 65536 | tf_op jit(solution)/shard_map/psum | solution.py:47
  335.3 11.7 %cholesky.324 = f32[128,128]{1,0:T(8,128)S(1)} custom-call(f32[128,128]{1,0:T(8,128)S(1)} %cholesky.428), custom_call_target="Cholesky" | custom-call | tf_op jit(solution)/shard_map/jit(cholesky)/cholesky | solution.py:15
  357.3 11.7 %cholesky.341 = f32[128,128]{1,0:T(8,128)S(1)} custom-call(f32[128,128]{1,0:T(8,128)S(1)} %convolution_subtract_fusion.5), custom_call_target="Cholesky" | custom-call | tf_op jit(solution)/shard_map/jit(cholesky)/cholesky | solution.py:15
  375.7 20.1 %custom-call.33 = f32[2,128,128]{1,2,0:T(8,128)S(1)} custom-call(f32[2,128,128]{2,1,0:T(8,128)S(1)} %get-tuple-element.75), custom_call_target="InvertDiagBlocksLowerTriangular" | custom-call | tf_op jit(solution)/shard_map/triangular_solve/custom-call.0 | solution.py:16
  402.9 11.7 %cholesky.358 = f32[128,128]{1,0:T(8,128)S(1)} custom-call(f32[128,128]{1,0:T(8,128)S(1)} %cholesky.431), custom_call_target="Cholesky" | custom-call | tf_op jit(solution)/shard_map/jit(cholesky)/cholesky | solution.py:15
  424.9 11.7 %cholesky.375 = f32[128,128]{1,0:T(8,128)S(1)} custom-call(f32[128,128]{1,0:T(8,128)S(1)} %convolution_subtract_fusion.3), custom_call_target="Cholesky" | custom-call | tf_op jit(solution)/shard_map/jit(cholesky)/cholesky | solution.py:15
  443.5 19.7 %custom-call.36 = f32[2,128,128]{1,2,0:T(8,128)S(1)} custom-call(f32[2,128,128]{2,1,0:T(8,128)S(1)} %get-tuple-element.77), custom_call_target="InvertDiagBlocksLowerTriangular" | custom-call | tf_op jit(solution)/shard_map/triangular_solve/custom-call.0 | solution.py:16
  468.9 30.9 %all_gather.10 = f32[256,256]{1,0:T(8,128)S(1)} all-gather(f32[32,256]{1,0:T(8,128)S(1)} %maximum_multiply_fusion.3), channel_id=1, replica_groups=mesh['row'=8,'col'=4] {'row'}, dimensions={0}, use_global_device_ids=true | all-gather | bytes 294912 | tf_op jit(solution)/shard_map/all_gather | solution.py:58
  505.5 10.0 %fusion.4 = f32[256,32,128]{2,0,1:T(8,128)} fusion(f32[32,128,256]{2,1,0:T(8,128)} %param.8, f32[256,256]{1,0:T(8,128)S(1)} %broadcast_divide_fusion), kind=kOutput, calls=%fused_computation.40 | convolution fusion | flops 3221225472 | bytes 8650752 | tf_op jit(solution)/shard_map/kij,jr->kir/dot_general | solution.py:60
  525.8 22.6 %all-reduce.12.cloned.1.call-done = f32[256,256]{0,1:T(8,128)} async-done(((f32[256,256]{0,1:T(8,128)}), f32[256,256]{0,1:T(8,128)}) %all-reduce.12.cloned.1.call-update) | async-done | bytes 262160 | tf_op jit(solution)/shard_map/psum | solution.py:32
  549.7 11.7 %cholesky.392 = f32[128,128]{1,0:T(8,128)S(1)} custom-call(f32[128,128]{1,0:T(8,128)S(1)} %cholesky.434), custom_call_target="Cholesky" | custom-call | tf_op jit(solution)/shard_map/jit(cholesky)/cholesky | solution.py:15
  571.7 11.7 %cholesky.409 = f32[128,128]{1,0:T(8,128)S(1)} custom-call(f32[128,128]{1,0:T(8,128)S(1)} %convolution_subtract_fusion.1), custom_call_target="Cholesky" | custom-call | tf_op jit(solution)/shard_map/jit(cholesky)/cholesky | solution.py:15
  590.2 19.9 %custom-call.39 = f32[2,128,128]{1,2,0:T(8,128)S(1)} custom-call(f32[2,128,128]{2,1,0:T(8,128)S(1)} %get-tuple-element.79), custom_call_target="InvertDiagBlocksLowerTriangular" | custom-call | tf_op jit(solution)/shard_map/triangular_solve/custom-call.0 | solution.py:16
  618.4 21.4 %psum.71 = f32[256]{0:T(256)S(1)} all-reduce(f32[256]{0:T(256)S(1)} %multiply_reduce_fusion.6), channel_id=1, replica_groups=mesh['row'=8,'col'=4] {'row'}, use_global_device_ids=true, to_apply=%region_20.24 | all-reduce | flops 256 | bytes 2048 | tf_op jit(solution)/shard_map/psum | solution.py:66
  (204 shorter events, 164.9 us)
Async XLA Ops:
  7.2 2.5 copy-start
  7.2 57.8 %all-reduce.8.cloned.1.call-start = ((), (), s32[]{:S(2)}) async-start(), calls=%async_computation.4 | async-start | bytes 524288 | tf_op jit(solution)/shard_map/psum | solution.py:43
  9.6 110.8 %all-reduce.6.cloned.1.call-start = ((), (), s32[]{:S(2)}) async-start(), calls=%async_computation.3 | async-start | bytes 524288 | tf_op jit(solution)/shard_map/psum | solution.py:41
  10.8 239.0 %reduce-scatter.10.cloned.1.call-start = ((), (), s32[]{:S(2)}) async-start(), calls=%async_computation.7 | async-start | bytes 294912
  120.4 67.6 %copy-start.1 = (f32[256,256]{0,1:T(8,128)S(1)}, f32[256,256]{0,1:T(8,128)}, u32[]{:S(2)}) copy-start(f32[256,256]{0,1:T(8,128)} %all-reduce.6.cloned.1.call-done) | copy-start | bytes 786436
  188.0 146.1 %all-reduce.10.cloned.1.call-start = ((), (), s32[]{:S(2)}) async-start(), calls=%async_computation.5 | async-start | bytes 524288 | tf_op jit(solution)/shard_map/psum | solution.py:32
  290.6 175.4 %reduce-scatter.12.cloned.1.call-start = ((), (), s32[]{:S(2)}) async-start(), calls=%async_computation.8 | async-start | bytes 294912
  397.2 118.2 %copy-start.3 = (f32[32,256]{1,0:T(8,128)}, f32[32,256]{1,0:T(8,128)S(1)}, u32[]{:S(2)}) copy-start(f32[32,256]{1,0:T(8,128)S(1)} %fusion.78) | copy-start | bytes 98308
  402.2 146.3 %all-reduce.12.cloned.1.call-start = ((), (), s32[]{:S(2)}) async-start(), calls=%async_computation.6 | async-start | bytes 524288 | tf_op jit(solution)/shard_map/psum | solution.py:32
  505.5 44.2 %copy-start.2 = (f32[256,256]{1,0:T(8,128)}, f32[256,256]{1,0:T(8,128)S(1)}, u32[]{:S(2)}) copy-start(f32[256,256]{1,0:T(8,128)S(1)} %broadcast_divide_fusion) | copy-start | bytes 786436
  516.8 93.4 %reduce-scatter.14.cloned.1.call-start = ((), (), s32[]{:S(2)}) async-start(), calls=%async_computation.9 | async-start | bytes 163840
  639.8 0.7 copy-start.4
Sparse Core Ops, SparseCore 0:
  10.9 34.9 all-reduce.7
  49.3 71.0 all-reduce.5
  188.1 61.6 reduce-scatter.9
  290.7 31.6 all-reduce.9
  402.3 63.6 reduce-scatter.11
  516.9 31.5 all-reduce.11
  551.5 19.8 reduce-scatter.13
where the time goes:
time: 653 us; the launch traced here: 648 us
  other arithmetic  290 us (44%)
  blocking collectives  182 us (28%)
  waiting for transfers between devices  81.9 us (13%)
  matrix products  46.5 us (7%)
  local copies, waits for them, and re-layouts  24.2 us (4%)
  between operations  21.7 us (3%)
    another operation x34, other arithmetic, solve_gram(): factor_lower = jnp.linalg.cholesky(hadamard)  172 us
    another operation x11, other arithmetic, solve_gram(): lax.linalg.triangular_solve(factor_lower, partials, left_side=False, lowe...  99.6 us
    psum x2, blocking collectives, body(): frame_sums = lax.psum(frame_terms, ('row', 'col'))  82.3 us
    all_gather x2, blocking collectives, body(): second_raw = lax.all_gather(solved_rows, 'row', axis=0, tiled=True)  61.7 us
    psum x1, waiting for transfers between devices, body(): first_gram = lax.psum(local_gram(initial_first), 'row') / rows_first  55.4 us
    psum x2, waiting for transfers between devices, normalize_second(): gram_new = lax.psum(local_gram(normed), 'col') / row_count  22.7 us
    another operation x39, local copies, waits for them, and re-layouts, solve_gram(): lax.linalg.triangular_solve(factor_lower, partials, left_side=False, lowe...  22 us
    psum x1, blocking collectives, body(): squares = lax.psum(jnp.sum(first_raw * first_raw, axis=0), 'row')  21.4 us
  transfers between devices with their start and end apart: 7, of which 4 were waited for; matrix products, arithmetic and copies ran while one was open for 32% of the time, Pallas kernels for 0%

commit v1 on v0

v1 whole, which is shorter than its diff:
```python
import functools
import math

import jax
import jax.numpy as jnp
from jax import lax
from jax.experimental import pallas as pl
from jax.experimental.pallas import tpu as pltpu
from jax.sharding import PartitionSpec as P

PASSES = 2
LANES = 128
PIVOTS = 8
MESH = pl.DeviceIdType.MESH
HIGHEST = lax.Precision.HIGHEST

epsilon = 1e-06


def product(a, b):
    return jnp.dot(a, b, precision=HIGHEST, preferred_element_type=jnp.float32)


def cross(a, b):
    return lax.dot_general(
        a, b, (((0,), (0,)), ((), ())), precision=HIGHEST, preferred_element_type=jnp.float32
    )


def invert(a, start, stop):
    size = a.shape[0]
    tiles = size // LANES
    row = lax.broadcasted_iota(jnp.int32, (PIVOTS, LANES), 0)
    lanes = [
        lax.broadcasted_iota(jnp.int32, (PIVOTS, LANES), 1) + q * LANES for q in range(tiles)
    ]
    wide = lax.broadcasted_iota(jnp.int32, (PIVOTS, size), 1)
    whole = lax.broadcasted_iota(jnp.int32, (size, size), 1)

    def step(g, carry):
        base = g * PIVOTS
        here = pl.ds(pl.multiple_of(base, PIVOTS), PIVOTS)
        rows = [a[here, q * LANES : (q + 1) * LANES] for q in range(tiles)]
        cols = []
        for t in range(PIVOTS):
            picked = sum(jnp.where(lanes[q] == base + t, rows[q], 0.0) for q in range(tiles))
            cols.append(
                jnp.broadcast_to(jnp.sum(picked, axis=1, keepdims=True), (PIVOTS, LANES))
            )
        work = []
        for q in range(tiles):
            place = lanes[q] - base
            inside = (place >= 0) & (place < PIVOTS)
            unit = jnp.where(place == row, 1.0, 0.0)
            work.append(jnp.where(inside, unit, rows[q]))
        for t in range(PIVOTS):
            pivot = 1.0 / jnp.broadcast_to(cols[t][t : t + 1, :], (PIVOTS, LANES))
            at = row == t

            def reduced(x):
                scaled = jnp.broadcast_to(x[t : t + 1, :], (PIVOTS, LANES)) * pivot
                return jnp.where(at, scaled, x - cols[t] * scaled)

            later = [reduced(cols[s]) for s in range(t + 1, PIVOTS)]
            work = [reduced(w) for w in work]
            cols[t + 1 :] = later
        solved = jnp.concatenate(work, axis=1)
        raw = a[here, :]
        inside = (wide >= base) & (wide < base + PIVOTS)
        left = jnp.where(inside, 0.0, jnp.where(wide < base, -raw, raw))
        kept = jnp.where((whole >= base) & (whole < base + PIVOTS), 0.0, a[...])
        a[...] = kept - cross(left, solved)
        a[here, :] = solved
        return carry

    lax.fori_loop(start, stop, step, 0)


def greet(sizes):
    barrier = pltpu.get_barrier_semaphore()
    for axis, n in sizes.items():
        me = lax.axis_index(axis)
        for d in range(1, n):
            pl.semaphore_signal(
                barrier, inc=1, device_id={axis: lax.rem(me + d, n)}, device_id_type=MESH
            )
    pl.semaphore_wait(barrier, sum(n - 1 for n in sizes.values()))


def scatter(axis, n, source, recv, sems):
    me = lax.axis_index(axis)
    chunk = recv.shape[1]
    copies = []
    for d in range(1, n):
        peer = lax.rem(me + d, n)
        copy = pltpu.make_async_remote_copy(
            src_ref=source.at[pl.ds(pl.multiple_of(peer * chunk, 8), chunk), :],
            dst_ref=recv.at[me],
            send_sem=sems.at[0, d - 1],
            recv_sem=sems.at[1, d - 1],
            device_id={axis: peer},
            device_id_type=MESH,
        )
        copy.start()
        copies.append(copy)
    recv[me] = source[pl.ds(pl.multiple_of(me * chunk, 8), chunk), :]
    return copies


def gather(axis, n, own, full, sems):
    me = lax.axis_index(axis)
    chunk = own.shape[0]
    place = pl.ds(pl.multiple_of(me * chunk, 8), chunk)
    full[place, :] = own
    copies = []
    for d in range(1, n):
        copy = pltpu.make_async_remote_copy(
            src_ref=full.at[place, :],
            dst_ref=full.at[place, :],
            send_sem=sems.at[0, d - 1],
            recv_sem=sems.at[1, d - 1],
            device_id={axis: lax.rem(me + d, n)},
            device_id_type=MESH,
        )
        copy.start()
        copies.append(copy)
    return copies


def finish(copies):
    for copy in copies:
        copy.wait()


def total(recv):
    result = recv[0]
    for s in range(1, recv.shape[0]):
        result = result + recv[s]
    return result


def total_blocks(full, n):
    chunk = full.shape[0] // n
    result = full[0:chunk, :]
    for s in range(1, n):
        result = result + full[s * chunk : (s + 1) * chunk, :]
    return result


def frames_of(sums, inverse, scale):
    raw = product(sums, inverse) * scale
    normed = raw / jnp.sqrt(jnp.mean(raw * raw, axis=0, keepdims=True) + epsilon)
    return normed, cross(normed, normed) / raw.shape[0]


def start_kernel(
    sizes, scales, gram1, gram2, terms, frames_out, frame_gram_out, first_gram_out,
    inv, recv1, recv2, full1, full2, parts1, parts2, s1, s2, s3, s4, s5, s6,
):
    row, col = sizes["row"], sizes["col"]
    greet(sizes)
    go1 = scatter("row", row, gram1, recv1, s1)
    go2 = scatter("col", col, gram2, recv2, s2)
    go3 = gather("row", row, terms[...], parts1, s3)
    finish(go2)
    go5 = gather("col", col, total(recv2), full2, s5)
    finish(go1)
    go4 = gather("row", row, total(recv1), full1, s4)
    finish(go3)
    go6 = gather("col", col, total_blocks(parts1, row), parts2, s6)
    finish(go4)
    finish(go5)
    first_gram = full1[...] * scales[0]
    first_gram_out[...] = first_gram
    inv[...] = first_gram * (full2[...] * scales[1])
    invert(inv, 0, inv.shape[0] // PIVOTS)
    finish(go6)
    normed, gram = frames_of(total_blocks(parts2, col), inv[...], scales[2])
    frames_out[...] = normed
    frame_gram_out[...] = gram


def frame_kernel(
    sizes, scales, first_gram, second_gram, terms, frames_out, frame_gram_out,
    inv, parts1, parts2, s1, s2,
):
    row, col = sizes["row"], sizes["col"]
    steps = inv.shape[0] // PIVOTS
    greet(sizes)
    go1 = gather("row", row, terms[...], parts1, s1)
    inv[...] = first_gram[...] * second_gram[...]
    invert(inv, 0, steps // 2)
    finish(go1)
    go2 = gather("col", col, total_blocks(parts1, row), parts2, s2)
    invert(inv, steps // 2, steps)
    finish(go2)
    normed, gram = frames_of(total_blocks(parts2, col), inv[...], scales[0])
    frames_out[...] = normed
    frame_gram_out[...] = gram


def second_kernel(
    sizes, scales, first_gram, frame_gram, terms, second_out, gram_out,
    inv, recv1, full1, local, recv2, full2, s1, s2, s3, s4,
):
    row, col = sizes["row"], sizes["col"]
    greet(sizes)
    go1 = scatter("row", row, terms, recv1, s1)
    inv[...] = first_gram[...] * frame_gram[...]
    invert(inv, 0, inv.shape[0] // PIVOTS)
    finish(go1)
    go2 = gather("row", row, product(total(recv1), inv[...]) * scales[0], full1, s2)
    finish(go2)
    raw = full1[...]
    local[...] = cross(raw, raw)
    go3 = scatter("col", col, local, recv2, s3)
    finish(go3)
    go4 = gather("col", col, total(recv2), full2, s4)
    finish(go4)
    gram = full2[...] * scales[1]
    size = gram.shape[0]
    down = lax.broadcasted_iota(jnp.int32, (size, size), 0)
    across = lax.broadcasted_iota(jnp.int32, (size, size), 1)
    diagonal = jnp.where(down == across, gram, 0.0)
    wide = jnp.sqrt(jnp.sum(diagonal, axis=0, keepdims=True) + epsilon)
    tall = jnp.sqrt(jnp.sum(diagonal, axis=1, keepdims=True) + epsilon)
    second_out[...] = raw / wide
    gram_out[...] = gram / wide / tall


def first_kernel(
    sizes, scales, second_gram, frame_gram, terms, first_out, weights_out,
    inv, recv1, full1, parts, s1, s2, s3,
):
    row, col = sizes["row"], sizes["col"]
    greet(sizes)
    go1 = scatter("col", col, terms, recv1, s1)
    inv[...] = second_gram[...] * frame_gram[...]
    invert(inv, 0, inv.shape[0] // PIVOTS)
    finish(go1)
    go2 = gather("col", col, product(total(recv1), inv[...]) * scales[0], full1, s2)
    finish(go2)
    raw = full1[...]
    squares = jnp.sum(raw * raw, axis=0, keepdims=True)
    go3 = gather("row", row, jnp.broadcast_to(squares, (8, raw.shape[1])), parts, s3)
    finish(go3)
    weights = jnp.sqrt(total_blocks(parts, row) * scales[1] + epsilon)
    weights_out[...] = weights
    first_out[...] = raw / weights[0:1, :]


def call(kernel, sizes, scales, args, outs, scratch, number, name):
    vmem = pl.BlockSpec(memory_space=pltpu.VMEM)
    return pl.pallas_call(
        functools.partial(kernel, sizes, scales),
        out_shape=[jax.ShapeDtypeStruct(shape, jnp.float32) for shape in outs],
        in_specs=[vmem] * len(args),
        out_specs=[vmem] * len(outs),
        scratch_shapes=scratch,
        compiler_params=pltpu.CompilerParams(
            collective_id=number, has_side_effects=True, vmem_limit_bytes=16 * 1024 * 1024
        ),
        name=name,
    )(*args)


def body(sizes, tensor, initial_first, initial_second):
    row, col = sizes["row"], sizes["col"]
    frames, own_first, own_second = tensor.shape
    rank = initial_first.shape[1]
    rows_first, rows_second = own_first * row, own_second * col
    square = (rank, rank)

    def vmem(*shape):
        return pltpu.VMEM(shape, jnp.float32)

    def sems(n):
        return pltpu.SemaphoreType.DMA((2, n - 1))

    def frame_terms(second):
        return jnp.einsum("kjr,jr->kr", contracted, second, precision=HIGHEST)

    gram1 = jnp.dot(initial_first.T, initial_first, precision=HIGHEST)
    gram2 = jnp.dot(initial_second.T, initial_second, precision=HIGHEST)
    contracted = jnp.einsum("kij,ir->kjr", tensor, initial_first, precision=HIGHEST)
    frame_scale = 1.0 / math.sqrt(rows_first * rows_second)
    second = initial_second
    for repeat in range(PASSES):
        terms = frame_terms(second)
        if repeat == 0:
            factor_frames, frame_gram, first_gram = call(
                start_kernel, sizes, (1.0 / rows_first, 1.0 / rows_second, frame_scale),
                (gram1, gram2, terms), ((frames, rank), square, square),
                [
                    vmem(*square), vmem(row, rank // row, rank), vmem(col, rank // col, rank),
                    vmem(*square), vmem(*square), vmem(row * frames, rank),
                    vmem(col * frames, rank),
                    sems(row), sems(col), sems(row), sems(row), sems(col), sems(col),
                ],
                0, "start",
            )
        else:
            factor_frames, frame_gram = call(
                frame_kernel, sizes, (frame_scale,), (first_gram, second_gram, terms),
                ((frames, rank), square),
                [
                    vmem(*square), vmem(row * frames, rank), vmem(col * frames, rank),
                    sems(row), sems(col),
                ],
                2 * repeat, "frame_%d" % repeat,
            )
        second_terms = jnp.einsum("kjr,kr->jr", contracted, factor_frames, precision=HIGHEST)
        second, second_gram = call(
            second_kernel, sizes, (1.0 / math.sqrt(rows_first * frames), 1.0 / rows_second),
            (first_gram, frame_gram, second_terms), ((own_second, rank), square),
            [
                vmem(*square), vmem(row, own_second // row, rank), vmem(own_second, rank),
                vmem(*square), vmem(col, rank // col, rank), vmem(*square),
                sems(row), sems(row), sems(col), sems(col),
            ],
            2 * repeat + 1, "second_%d" % repeat,
        )
    second_contracted = jnp.einsum("kij,jr->kir", tensor, second, precision=HIGHEST)
    first_terms = jnp.einsum("kir,kr->ir", second_contracted, factor_frames, precision=HIGHEST)
    factor_first, weights = call(
        first_kernel, sizes, (1.0 / math.sqrt(rows_second * frames), 1.0 / rows_first),
        (second_gram, frame_gram, first_terms), ((own_first, rank), (8, rank)),
        [
            vmem(*square), vmem(col, own_first // col, rank), vmem(own_first, rank),
            vmem(row * 8, rank), sems(col), sems(col), sems(row),
        ],
        2 * PASSES, "first",
    )
    return (factor_first, second, factor_frames, weights[0])


def solution(mesh):
    sizes = {"row": mesh.shape["row"], "col": mesh.shape["col"]}
    placed = (P(None, "row", "col"), P("row", None), P("col", None))
    return jax.shard_map(
        functools.partial(body, sizes),
        mesh=mesh,
        in_specs=placed,
        out_specs=(P("row", None), P("col", None), P(), P()),
        check_vma=False,
    )
```

time: 653 us -> 190 us (0.29)
  other arithmetic: 290 us -> 7.68 us
  blocking collectives: 182 us -> 0 us
  Pallas kernels: 0 us -> 158 us
  waiting for transfers between devices: 81.9 us -> 0 us
  matrix products: 46.5 us -> 19.8 us
  between operations: 21.7 us -> 0.75 us
  local copies, waits for them, and re-layouts: 24.2 us -> 3.63 us
    another operation x45 -> x0, other arithmetic: 272 us -> none  [the longest x34 172 us: solve_gram(): factor_lower = jnp.linalg.cholesky(hadamard)]
    pallas_call x0 -> x5, Pallas kernels: none -> 158 us  [call(): pl.pallas_call(functools.partial(kernel, sizes, scales), out_shape=[jax.S...]
    psum x5 -> x0, blocking collectives: 115 us -> none  [the longest x2 82.3 us: body(): frame_sums = lax.psum(frame_terms, ('row', 'col'))]
    psum x4 -> x0, waiting for transfers between devices: 78.1 us -> none  [the longest x1 55.4 us: body(): first_gram = lax.psum(local_gram(initial_first), 'row') / rows_first]
    all_gather x3 -> x0, blocking collectives: 67.2 us -> none  [the longest x2 61.7 us: body(): second_raw = lax.all_gather(solved_rows, 'row', axis=0, tiled=True)]
    another operation x49 -> x0, local copies, waits for them, and re-layouts: 22.1 us -> none  [the longest x39 22 us: solve_gram(): lax.linalg.triangular_solve(factor_lower, partials, left_side=False, lowe...]
    dot_general x9 -> x4, matrix products: 35.8 us -> 19.8 us  [the longest x1 9.17 us: body(): jnp.einsum('kij,ir->kjr', tensor, initial_first, precision=HIGHEST)]
    another operation x40 -> x0, matrix products: 10.7 us -> none  [the longest x15 5.31 us: solve_gram(): lax.linalg.triangular_solve(factor_lower, partials, left_side=False, lowe...]
  transfers between devices with their start and end apart: 7 -> 0, of which waited for: 4 -> 0; matrix products, arithmetic and copies ran while one was open for 32% -> 0% of each run, Pallas kernels for 0% -> 0%
where the time goes in v1:
time: 190 us
  Pallas kernels  158 us (83%)
  matrix products  19.8 us (10%)
  other arithmetic  7.68 us (4%)
  local copies, waits for them, and re-layouts  3.63 us (2%)
    pallas_call x5, Pallas kernels, call(): pl.pallas_call(functools.partial(kernel, sizes, scales), out_shape=[jax.S...  158 us
    dot_general x1, matrix products, body(): jnp.einsum('kij,ir->kjr', tensor, initial_first, precision=HIGHEST)  9.17 us
    dot_general x1, matrix products, body(): jnp.einsum('kij,jr->kir', tensor, second, precision=HIGHEST)  8.61 us
    unnamed x1, other arithmetic  4.85 us

profile of v1, /device:TPU:0, one launch (start us, length us, event | category | flops | bytes accessed | tf_op | source)
XLA Modules:
  0.0 190.1 jit_solution(12610988335320817432)
XLA Ops:
  0.6 0.0 copy-start
  0.6 0.9 copy-done
  1.5 0.4 fusion.5.gram1
  2.0 1.7 fusion.6.gram2
  3.6 9.2 %multiply_reduce_fusion.3 = (f32[256,32]{0,1:T(8,128)S(1)}, f32[32,256,256]{2,1,0:T(8,128)S(1)}) fusion(f32[256,256]{0,1:T(8,128)} %bitcast.45, f32[32,128,256]{2,1,0:T(8,128)} %param.3, f32[128,256]{1,0:T(8,128)S(1)} %copy-done), kind=kOutput, calls=%fused_computation.3 | convolution fusion | flops 3225411584 | bytes 13008896 | tf_op jit(solution)/shard_map/kij,ir->kjr/dot_general | solution.py:285
  12.8 40.7 %start.1 = (f32[32,256]{1,0:T(8,128)S(1)}, f32[256,256]{1,0:T(8,128)S(1)}, f32[256,256]{1,0:T(8,128)S(1)}) custom-call(f32[256,256]{1,0:T(8,128)S(1)} %fusion.5.gram1, f32[256,256]{1,0:T(8,128)S(1)} %fusion.6.gram2, f32[32,256]{1,0:T(8,128)S(1)} %bitcast.42), custom_call_target="tpu_custom_call" | custom-call | tf_op jit(solution)/shard_map/start/pallas_call | solution.py:254
  53.5 1.0 multiply_reduce_fusion.2
  54.5 34.2 %second_0.1 = (f32[256,256]{1,0:T(8,128)S(1)}, f32[256,256]{1,0:T(8,128)S(1)}) custom-call(f32[256,256]{1,0:T(8,128)S(1)} %get-tuple-element.15.first_gram, f32[256,256]{1,0:T(8,128)S(1)} %get-tuple-element.16.frame_gram, f32[256,256]{1,0:T(8,128)S(1)} %bitcast.36), custom_call_target="tpu_custom_call" | custom-call | tf_op jit(solution)/shard_map/second_0/pallas_call | solution.py:254
  88.7 0.8 multiply_reduce_fusion.1
  89.5 21.4 %frame_1.1 = (f32[32,256]{1,0:T(8,128)S(1)}, f32[256,256]{1,0:T(8,128)S(1)}) custom-call(f32[256,256]{1,0:T(8,128)S(1)} %get-tuple-element.15.first_gram, f32[256,256]{1,0:T(8,128)S(1)} %get-tuple-element.18.second_gram, f32[32,256]{1,0:T(8,128)S(1)} %bitcast.43), custom_call_target="tpu_custom_call" | custom-call | tf_op jit(solution)/shard_map/frame_1/pallas_call | solution.py:254
  111.0 1.0 multiply_reduce_fusion
  112.0 33.8 %second_1.1 = (f32[256,256]{1,0:T(8,128)S(1)}, f32[256,256]{1,0:T(8,128)S(1)}) custom-call(f32[256,256]{1,0:T(8,128)S(1)} %get-tuple-element.15.first_gram, f32[256,256]{1,0:T(8,128)S(1)} %get-tuple-element.20.frame_gram, f32[256,256]{1,0:T(8,128)S(1)} %bitcast.37), custom_call_target="tpu_custom_call" | custom-call | tf_op jit(solution)/shard_map/second_1/pallas_call | solution.py:254
  145.8 0.1 copy.45
  145.9 8.6 %fusion.1 = f32[256,32,128]{2,0,1:T(8,128)S(1)} fusion(f32[32,128,256]{2,1,0:T(8,128)} %param.3, f32[256,256]{1,0:T(8,128)S(1)} %get-tuple-element.33), kind=kOutput, calls=%fused_computation.6 | convolution fusion | flops 3221225472 | bytes 8650752 | tf_op jit(solution)/shard_map/kij,jr->kir/dot_general | solution.py:323
  154.5 4.9 %fusion = f32[256,128]{1,0:T(8,128)S(1)} fusion(f32[256,32,128]{2,0,1:T(8,128)S(1)} %fusion.1, f32[256,32]{1,0:T(8,128)S(1)} %copy.45), kind=kLoop, calls=%fused_computation.5 | loop fusion | flops 2064384 | bytes 4358144
  159.3 0.1 copy.39
  159.4 28.1 %first.1 = (f32[128,256]{1,0:T(8,128)S(1)}, f32[8,256]{1,0:T(8,128)S(1)}) custom-call(f32[256,256]{1,0:T(8,128)S(1)} %get-tuple-element.22.second_gram, f32[256,256]{1,0:T(8,128)S(1)} %get-tuple-element.20.frame_gram, f32[128,256]{1,0:T(8,128)S(1)} %bitcast.38), custom_call_target="tpu_custom_call" | custom-call | tf_op jit(solution)/shard_map/first/pallas_call | solution.py:254
  187.6 0.6 slice.3
  188.2 0.7 copy.52
  188.8 0.7 copy.53
  189.5 0.6 copy.54
Async XLA Ops:
  0.6 0.9 copy-start

commit v2 on v1

v2 whole, which is shorter than its diff:
```python
import functools
import math

import jax
import jax.numpy as jnp
from jax import lax
from jax.experimental import pallas as pl
from jax.experimental.pallas import tpu as pltpu
from jax.sharding import PartitionSpec as P

PASSES = 2
LANES = 128
PIVOTS = 16
MESH = pl.DeviceIdType.MESH
HIGHEST = lax.Precision.HIGHEST

epsilon = 1e-06


def product(a, b):
    return jnp.dot(a, b, precision=HIGHEST, preferred_element_type=jnp.float32)


def cross(a, b):
    return lax.dot_general(
        a, b, (((0,), (0,)), ((), ())), precision=HIGHEST, preferred_element_type=jnp.float32
    )


def invert(a, start, stop):
    size = a.shape[0]
    tiles = size // LANES
    row = lax.broadcasted_iota(jnp.int32, (PIVOTS, LANES), 0)
    lanes = [
        lax.broadcasted_iota(jnp.int32, (PIVOTS, LANES), 1) + q * LANES for q in range(tiles)
    ]
    wide = lax.broadcasted_iota(jnp.int32, (PIVOTS, size), 1)
    whole = lax.broadcasted_iota(jnp.int32, (size, size), 1)

    def step(g, carry):
        base = g * PIVOTS
        here = pl.ds(pl.multiple_of(base, PIVOTS), PIVOTS)
        rows = [a[here, q * LANES : (q + 1) * LANES] for q in range(tiles)]
        cols = []
        for t in range(PIVOTS):
            picked = sum(jnp.where(lanes[q] == base + t, rows[q], 0.0) for q in range(tiles))
            cols.append(
                jnp.broadcast_to(jnp.sum(picked, axis=1, keepdims=True), (PIVOTS, LANES))
            )
        work = []
        for q in range(tiles):
            place = lanes[q] - base
            inside = (place >= 0) & (place < PIVOTS)
            unit = jnp.where(place == row, 1.0, 0.0)
            work.append(jnp.where(inside, unit, rows[q]))
        for t in range(PIVOTS):
            pivot = 1.0 / jnp.broadcast_to(cols[t][t : t + 1, :], (PIVOTS, LANES))
            at = row == t

            def reduced(x):
                scaled = jnp.broadcast_to(x[t : t + 1, :], (PIVOTS, LANES)) * pivot
                return jnp.where(at, scaled, x - cols[t] * scaled)

            later = [reduced(cols[s]) for s in range(t + 1, PIVOTS)]
            work = [reduced(w) for w in work]
            cols[t + 1 :] = later
        solved = jnp.concatenate(work, axis=1)
        raw = a[here, :]
        inside = (wide >= base) & (wide < base + PIVOTS)
        left = jnp.where(inside, 0.0, jnp.where(wide < base, -raw, raw))
        kept = jnp.where((whole >= base) & (whole < base + PIVOTS), 0.0, a[...])
        a[...] = kept - cross(left, solved)
        a[here, :] = solved
        return carry

    lax.fori_loop(start, stop, step, 0)


def greet(sizes):
    barrier = pltpu.get_barrier_semaphore()
    for axis, n in sizes.items():
        me = lax.axis_index(axis)
        for d in range(1, n):
            pl.semaphore_signal(
                barrier, inc=1, device_id={axis: lax.rem(me + d, n)}, device_id_type=MESH
            )
    pl.semaphore_wait(barrier, sum(n - 1 for n in sizes.values()))


def scatter(axis, n, source, recv, sems):
    me = lax.axis_index(axis)
    chunk = recv.shape[1]
    copies = []
    for d in range(1, n):
        peer = lax.rem(me + d, n)
        copy = pltpu.make_async_remote_copy(
            src_ref=source.at[pl.ds(pl.multiple_of(peer * chunk, 8), chunk), :],
            dst_ref=recv.at[me],
            send_sem=sems.at[0, d - 1],
            recv_sem=sems.at[1, d - 1],
            device_id={axis: peer},
            device_id_type=MESH,
        )
        copy.start()
        copies.append(copy)
    recv[me] = source[pl.ds(pl.multiple_of(me * chunk, 8), chunk), :]
    return copies


def gather(axis, n, own, full, sems):
    me = lax.axis_index(axis)
    chunk = own.shape[0]
    place = pl.ds(pl.multiple_of(me * chunk, 8), chunk)
    full[place, :] = own
    copies = []
    for d in range(1, n):
        copy = pltpu.make_async_remote_copy(
            src_ref=full.at[place, :],
            dst_ref=full.at[place, :],
            send_sem=sems.at[0, d - 1],
            recv_sem=sems.at[1, d - 1],
            device_id={axis: lax.rem(me + d, n)},
            device_id_type=MESH,
        )
        copy.start()
        copies.append(copy)
    return copies


def finish(copies):
    for copy in copies:
        copy.wait()


def total(recv):
    result = recv[0]
    for s in range(1, recv.shape[0]):
        result = result + recv[s]
    return result


def total_blocks(full, n):
    chunk = full.shape[0] // n
    result = full[0:chunk, :]
    for s in range(1, n):
        result = result + full[s * chunk : (s + 1) * chunk, :]
    return result


def layout(sizes, frames, own_first, own_second, rank):
    row, col = sizes["row"], sizes["col"]
    square = (rank, rank)
    buffers = {
        "tens": (frames, own_first, own_second),
        "held": (frames, own_second, rank),
        "inv": square, "sums": (frames, rank),
        "gram_a": square, "recv_a": (row, rank // row, rank), "full_a": square,
        "gram_b": square, "recv_b": (col, rank // col, rank), "full_b": square,
        "terms_f": (own_first, rank), "recv_f": (col, own_first // col, rank),
        "raw_f": (own_first, rank), "parts_w": (row * 8, rank),
    }
    axes = {"a": row, "a2": row, "b": col, "b2": col, "f": col, "f2": col, "w": row}
    for p in range(PASSES):
        buffers.update({
            "parts_r%d" % p: (row * frames, rank), "parts_c%d" % p: (col * frames, rank),
            "terms_s%d" % p: (own_second, rank),
            "recv_s%d" % p: (row, own_second // row, rank), "raw_s%d" % p: (own_second, rank),
            "gram_g%d" % p: square, "recv_g%d" % p: (col, rank // col, rank),
            "full_g%d" % p: square,
        })
        axes.update({
            "r%d" % p: row, "c%d" % p: col, "s%d" % p: row, "t%d" % p: row,
            "g%d" % p: col, "h%d" % p: col,
        })
    names = list(buffers) + ["sem_" + name for name in axes] + ["sem_load"]
    shapes = [pltpu.VMEM(shape, jnp.float32) for shape in buffers.values()]
    shapes += [pltpu.SemaphoreType.DMA((2, n - 1)) for n in axes.values()]
    shapes += [pltpu.SemaphoreType.DMA((frames,))]
    return names, shapes


def kernel(sizes, names, tensor, first, second, first_out, second_out, frames_out, weights_out, *scratch):
    row, col = sizes["row"], sizes["col"]
    v = dict(zip(names, scratch))
    inv, sums, tens, held = v["inv"], v["sums"], v["tens"], v["held"]
    frames, own_first, own_second = tensor.shape
    rank = first.shape[1]
    rows_first, rows_second = own_first * row, own_second * col
    steps = rank // PIVOTS

    def load(k):
        return pltpu.make_async_copy(tensor.at[k], tens.at[k], v["sem_load"].at[k])

    def start_load(k, carry):
        load(k).start()
        return carry

    def contract(start, stop):
        def step(k, carry):
            load(k).wait()
            part = cross(tens[k], first[...])
            held[k] = part
            sums[pl.ds(k, 1), :] = jnp.sum(part * second[...], axis=0, keepdims=True)
            return carry

        lax.fori_loop(start, stop, step, 0)

    def frame_terms(raw):
        def step(k, carry):
            sums[pl.ds(k, 1), :] = jnp.sum(held[k] * raw[...], axis=0, keepdims=True)
            return carry

        lax.fori_loop(0, frames, step, 0)

    def second_terms(out):
        block = math.gcd(own_second, 64)
        for c in range(0, own_second, block):
            def step(k, total):
                return total + held[k, c : c + block, :] * frames_out[pl.ds(k, 1), :]

            out[c : c + block, :] = lax.fori_loop(
                0, frames, step, jnp.zeros((block, rank), jnp.float32), unroll=4
            )

    def first_terms(raw, start, stop):
        def step(k, carry):
            part = product(tens[k], raw[...])
            v["terms_f"][...] += part * frames_out[pl.ds(k, 1), :]
            return carry

        lax.fori_loop(start, stop, step, 0)

    def solve_frames(frame_sums):
        raw = product(frame_sums, inv[...]) * (1.0 / math.sqrt(rows_first * rows_second))
        normed = raw / jnp.sqrt(jnp.mean(raw * raw, axis=0, keepdims=True) + epsilon)
        frames_out[...] = normed
        return cross(normed, normed) / frames

    lax.fori_loop(0, frames, start_load, 0)
    v["gram_a"][...] = cross(first[...], first[...])
    v["gram_b"][...] = cross(second[...], second[...])
    greet(sizes)
    go_a = scatter("row", row, v["gram_a"], v["recv_a"], v["sem_a"])
    go_b = scatter("col", col, v["gram_b"], v["recv_b"], v["sem_b"])
    contract(0, frames // 2)
    finish(go_a)
    go_a = gather("row", row, total(v["recv_a"]), v["full_a"], v["sem_a2"])
    finish(go_b)
    go_b = gather("col", col, total(v["recv_b"]), v["full_b"], v["sem_b2"])
    contract(frames // 2, frames)
    finish(go_a)
    finish(go_b)
    first_gram = v["gram_a"]
    first_gram[...] = v["full_a"][...] * (1.0 / rows_first)
    second_gram = v["full_b"][...] * (1.0 / rows_second)
    wide = None
    for p in range(PASSES):
        here = str(p)
        if p == 0:
            go_r = gather("row", row, sums[...], v["parts_r0"], v["sem_r0"])
            inv[...] = first_gram[...] * second_gram
            invert(inv, 0, steps // 2)
            finish(go_r)
            go_c = gather(
                "col", col, total_blocks(v["parts_r0"], row), v["parts_c0"], v["sem_c0"]
            )
            invert(inv, steps // 2, steps)
        else:
            inv[...] = first_gram[...] * second_gram
            invert(inv, 0, steps)
        finish(go_c)
        frame_sums = total_blocks(v["parts_c" + here], col)
        if wide is not None:
            frame_sums = frame_sums / wide
        frame_gram = solve_frames(frame_sums)
        second_terms(v["terms_s" + here])
        go_s = scatter(
            "row", row, v["terms_s" + here], v["recv_s" + here], v["sem_s" + here]
        )
        inv[...] = first_gram[...] * frame_gram
        invert(inv, 0, steps)
        finish(go_s)
        solved = product(total(v["recv_s" + here]), inv[...])
        raw = v["raw_s" + here]
        go_s = gather(
            "row", row, solved * (1.0 / math.sqrt(rows_first * frames)), raw, v["sem_t" + here]
        )
        finish(go_s)
        v["gram_g" + here][...] = cross(raw[...], raw[...])
        go_g = scatter(
            "col", col, v["gram_g" + here], v["recv_g" + here], v["sem_g" + here]
        )
        last = p + 1 == PASSES
        if last:
            v["terms_f"][...] = jnp.zeros((own_first, rank), jnp.float32)
            first_terms(raw, 0, frames // 2)
        else:
            later = str(p + 1)
            frame_terms(raw)
            go_r = gather("row", row, sums[...], v["parts_r" + later], v["sem_r" + later])
        finish(go_g)
        go_g = gather(
            "col", col, total(v["recv_g" + here]), v["full_g" + here], v["sem_h" + here]
        )
        if last:
            first_terms(raw, frames // 2, frames)
            go_f = scatter("col", col, v["terms_f"], v["recv_f"], v["sem_f"])
        else:
            finish(go_r)
            go_c = gather(
                "col", col, total_blocks(v["parts_r" + later], row),
                v["parts_c" + later], v["sem_c" + later],
            )
        finish(go_g)
        gram = v["full_g" + here][...] * (1.0 / rows_second)
        down = lax.broadcasted_iota(jnp.int32, (rank, rank), 0)
        across = lax.broadcasted_iota(jnp.int32, (rank, rank), 1)
        diagonal = jnp.where(down == across, gram, 0.0)
        wide = jnp.sqrt(jnp.sum(diagonal, axis=0, keepdims=True) + epsilon)
        tall = jnp.sqrt(jnp.sum(diagonal, axis=1, keepdims=True) + epsilon)
        second_gram = gram / wide / tall
    inv[...] = second_gram * frame_gram
    second_out[...] = raw[...] / wide
    invert(inv, 0, steps)
    finish(go_f)
    solved = product(total(v["recv_f"]) / wide, inv[...])
    go_f = gather(
        "col", col, solved * (1.0 / math.sqrt(rows_second * frames)), v["raw_f"], v["sem_f2"]
    )
    finish(go_f)
    raw = v["raw_f"][...]
    squares = jnp.sum(raw * raw, axis=0, keepdims=True)
    go_w = gather("row", row, jnp.broadcast_to(squares, (8, rank)), v["parts_w"], v["sem_w"])
    finish(go_w)
    weights = jnp.sqrt(total_blocks(v["parts_w"], row) * (1.0 / rows_first) + epsilon)
    weights_out[...] = weights
    first_out[...] = raw / weights[0:1, :]


def body(sizes, tensor, initial_first, initial_second):
    frames, own_first, own_second = tensor.shape
    rank = initial_first.shape[1]
    names, scratch = layout(sizes, frames, own_first, own_second, rank)
    vmem = pl.BlockSpec(memory_space=pltpu.VMEM)
    outs = ((own_first, rank), (own_second, rank), (frames, rank), (8, rank))
    factor_first, second, factor_frames, weights = pl.pallas_call(
        functools.partial(kernel, sizes, names),
        out_shape=[jax.ShapeDtypeStruct(shape, jnp.float32) for shape in outs],
        in_specs=[pl.BlockSpec(memory_space=pl.ANY), vmem, vmem],
        out_specs=[vmem] * len(outs),
        scratch_shapes=scratch,
        compiler_params=pltpu.CompilerParams(
            collective_id=0, has_side_effects=True, vmem_limit_bytes=48 * 1024 * 1024
        ),
        name="als",
    )(tensor, initial_first, initial_second)
    return (factor_first, second, factor_frames, weights[0])


def solution(mesh):
    sizes = {"row": mesh.shape["row"], "col": mesh.shape["col"]}
    placed = (P(None, "row", "col"), P("row", None), P("col", None))
    return jax.shard_map(
        functools.partial(body, sizes),
        mesh=mesh,
        in_specs=placed,
        out_specs=(P("row", None), P("col", None), P(), P()),
        check_vma=False,
    )
```

time: 190 us -> 133 us (0.70)
  Pallas kernels: 158 us -> 125 us
  matrix products: 19.8 us -> 0 us
  other arithmetic: 7.68 us -> 0 us
  local copies, waits for them, and re-layouts: 3.63 us -> 6.57 us
    pallas_call x5 -> x1, Pallas kernels: 158 us -> 125 us  [body(): pl.pallas_call(functools.partial(kernel, sizes, names), out_shape=[jax.Sh...]
    dot_general x4 -> x0, matrix products: 19.8 us -> none  [the longest x1 9.17 us: body(): jnp.einsum('kij,ir->kjr', tensor, initial_first, precision=HIGHEST)]
    unnamed x1 -> x0, other arithmetic: 4.85 us -> none
    unnamed x6 -> x9, local copies, waits for them, and re-layouts: 2.97 us -> 6.01 us
    dot_general x3 -> x0, other arithmetic: 2.82 us -> none  [the longest x2 2.01 us: body(): jnp.einsum('kjr,kr->jr', contracted, factor_frames, precision=HIGHEST)]
where the time goes in v2:
time: 133 us
  Pallas kernels  125 us (94%)
  local copies, waits for them, and re-layouts  6.57 us (5%)
    pallas_call x1, Pallas kernels, body(): pl.pallas_call(functools.partial(kernel, sizes, names), out_shape=[jax.Sh...  125 us
    unnamed x9, local copies, waits for them, and re-layouts  6.01 us

profile of v2, /device:TPU:0, one launch (start us, length us, event | category | flops | bytes accessed | tf_op | source)
XLA Modules:
  0.0 132.5 jit_solution(9056279774589480784)
XLA Ops:
  0.6 0.0 copy-start
  0.6 2.2 %copy-done = f32[32,128,256]{2,1,0:T(8,128)S(1)} copy-done((f32[32,128,256]{2,1,0:T(8,128)S(1)}, f32[32,128,256]{2,1,0:T(8,128)}, u32[]{:S(2)}) %copy-start) | copy-done | bytes 4194328
  2.8 0.0 copy-start.1
  2.8 0.9 copy-done.1
  3.8 0.0 copy-start.2
  3.8 0.9 copy-done.2
  4.7 125.3 %als.1 = (f32[128,256]{1,0:T(8,128)S(1)}, f32[256,256]{1,0:T(8,128)S(1)}, f32[32,256]{1,0:T(8,128)S(1)}, f32[8,256]{1,0:T(8,128)S(1)}) custom-call(f32[32,128,256]{2,1,0:T(8,128)S(1)} %copy-done, f32[128,256]{1,0:T(8,128)S(1)} %copy-done.2, f32[256,256]{1,0:T(8,128)S(1)} %copy-done.1), custom_call_target="tpu_custom_call" | custom-call | tf_op jit(solution)/shard_map/als/pallas_call | solution.py:346
  130.0 0.6 slice.3
  130.6 0.7 copy.10
  131.2 0.7 copy.11
  131.9 0.6 copy.12
Async XLA Ops:
  0.6 2.2 %copy-start = (f32[32,128,256]{2,1,0:T(8,128)S(1)}, f32[32,128,256]{2,1,0:T(8,128)}, u32[]{:S(2)}) copy-start(f32[32,128,256]{2,1,0:T(8,128)} %tensor.1) | copy-start | bytes 12582916
  2.8 0.9 copy-start.1
  3.8 0.9 copy-start.2

commit v3 on v2

--- a/solution.py
+++ b/solution.py
@@ -196,14 +196,19 @@
         return carry
 
     def contract(start, stop):
-        def step(k, carry):
-            load(k).wait()
-            part = cross(tens[k], first[...])
-            held[k] = part
-            sums[pl.ds(k, 1), :] = jnp.sum(part * second[...], axis=0, keepdims=True)
+        group = math.gcd(stop - start, 4)
+
+        def step(g, carry):
+            ks = [start + g * group + u for u in range(group)]
+            for k in ks:
+                load(k).wait()
+            parts = [cross(tens[k], first[...]) for k in ks]
+            for k, part in zip(ks, parts):
+                held[k] = part
+                sums[pl.ds(k, 1), :] = jnp.sum(part * second[...], axis=0, keepdims=True)
             return carry
 
-        lax.fori_loop(start, stop, step, 0)
+        lax.fori_loop(0, (stop - start) // group, step, 0)
 
     def frame_terms(raw):
         def step(k, carry):
@@ -223,12 +228,19 @@
             )
 
     def first_terms(raw, start, stop):
-        def step(k, carry):
-            part = product(tens[k], raw[...])
-            v["terms_f"][...] += part * frames_out[pl.ds(k, 1), :]
+        group = math.gcd(stop - start, 4)
+
+        def step(g, carry):
+            base = start + g * group
+            stacked = tens[pl.ds(base, group)].reshape(group * own_first, own_second)
+            part = product(stacked, raw[...])
+            v["terms_f"][...] += sum(
+                part[u * own_first : (u + 1) * own_first, :] * frames_out[pl.ds(base + u, 1), :]
+                for u in range(group)
+            )
             return carry
 
-        lax.fori_loop(start, stop, step, 0)
+        lax.fori_loop(0, (stop - start) // group, step, 0)
 
     def solve_frames(frame_sums):
         raw = product(frame_sums, inv[...]) * (1.0 / math.sqrt(rows_first * rows_second))

time: 133 us -> 131 us (0.985)
    pallas_call x1, Pallas kernels: 125 us -> 124 us  [body(): pl.pallas_call(functools.partial(kernel, sizes, names), out_shape=[jax.Sh...]
where the time goes in v3:
time: 131 us
  Pallas kernels  124 us (95%)
  local copies, waits for them, and re-layouts  6.57 us (5%)
    pallas_call x1, Pallas kernels, body(): pl.pallas_call(functools.partial(kernel, sizes, names), out_shape=[jax.Sh...  124 us
    unnamed x9, local copies, waits for them, and re-layouts  6.01 us

profile of v3, /device:TPU:0, one launch (start us, length us, event | category | flops | bytes accessed | tf_op | source)
XLA Modules:
  0.0 130.8 jit_solution(10077121806767231288)
XLA Ops:
  0.6 0.0 copy-start
  0.6 2.2 %copy-done = f32[32,128,256]{2,1,0:T(8,128)S(1)} copy-done((f32[32,128,256]{2,1,0:T(8,128)S(1)}, f32[32,128,256]{2,1,0:T(8,128)}, u32[]{:S(2)}) %copy-start) | copy-done | bytes 4194328
  2.8 0.0 copy-start.1
  2.8 0.9 copy-done.1
  3.8 0.0 copy-start.2
  3.8 0.9 copy-done.2
  4.7 123.5 %als.1 = (f32[128,256]{1,0:T(8,128)S(1)}, f32[256,256]{1,0:T(8,128)S(1)}, f32[32,256]{1,0:T(8,128)S(1)}, f32[8,256]{1,0:T(8,128)S(1)}) custom-call(f32[32,128,256]{2,1,0:T(8,128)S(1)} %copy-done, f32[128,256]{1,0:T(8,128)S(1)} %copy-done.2, f32[256,256]{1,0:T(8,128)S(1)} %copy-done.1), custom_call_target="tpu_custom_call" | custom-call | tf_op jit(solution)/shard_map/als/pallas_call | solution.py:358
  128.2 0.6 slice.3
  128.8 0.7 copy.10
  129.4 0.7 copy.11
  130.1 0.6 copy.12
Async XLA Ops:
  0.6 2.2 %copy-start = (f32[32,128,256]{2,1,0:T(8,128)S(1)}, f32[32,128,256]{2,1,0:T(8,128)}, u32[]{:S(2)}) copy-start(f32[32,128,256]{2,1,0:T(8,128)} %tensor.1) | copy-start | bytes 12582916
  2.8 0.9 copy-start.1
  3.8 0.9 copy-start.2
